TPU v7x, 32 devices: a whole 2x2x4 slice. The times are simulated.
32 devices in a mesh: section: 2 (over y), mp: 16 (over z, x, core).
Axes of the slice: x: 2, y: 2, z: 4, core: 2. Of those that a mesh axis runs over, the one named last changes fastest.
Arguments:
- features: bfloat16 [4, 32, 8192], P(None, None, 'mp'), may hold values from -6 to 6
- labels: int32 [4, 32], replicated, may hold values 0 or 1
- weights: bfloat16 [2, 8192, 8192], P('section', None, 'mp'), may hold values from -1.78986404 to 1.78986404
- vectors: float32 [2, 8192], P('section', 'mp'), may hold values from -6 to 6
- head_weight: float32 [8192], P('mp'), may hold values from -0.0625 to 0.0625
Outputs:
- weight_grad: bfloat16 [2, 8192, 8192], P('section', None, 'mp')
- new_vectors: float32 [2, 8192], P('section', 'mp')
- rank_coef: float32 [2], P('section')
All inputs are finite; a program needn't handle non-finite values.
Results may differ from a plain program's by a relative error of at most 0.015.
Values may be sent and summed in bfloat16 or wider, within the bound.
No kernel may reach another device: no remote copies, remote signals or barrier semaphores. Data moves between devices by JAX's collectives and lax.ppermute only.
A program may use at most 64 MiB of HBM per device.

v0:
```python
import jax
import jax.numpy as jnp
from jax import lax
from jax.sharding import PartitionSpec as P

loss_scale = 32.0
tiny_eps = 1e-06


def shifted(block, axis, distance):
    devices = range(lax.axis_size(axis))
    route = [(i - distance, i) for i in devices if i - distance in devices]
    return lax.ppermute(block, axis, route)


def silu_slope(pre_act):
    gate_val = jax.nn.sigmoid(pre_act)
    return gate_val * (1.0 + pre_act * (1.0 - gate_val))


def keep_slot(stored, update, micro_slot, is_live):
    previous = lax.dynamic_index_in_dim(stored, micro_slot, 0, keepdims=False)
    return lax.dynamic_update_index_in_dim(
        stored, jnp.where(is_live, update, previous), micro_slot, 0
    )


def power_step(weight, vector_u):
    vector_bf = vector_u.astype(jnp.bfloat16)
    left_sum = lax.psum(jnp.dot(weight, vector_bf, preferred_element_type=jnp.float32), "mp")
    vector_v = (left_sum * lax.rsqrt(jnp.sum(left_sum * left_sum) + tiny_eps)).astype(jnp.bfloat16)
    right_part = jnp.dot(vector_v, weight, preferred_element_type=jnp.float32)
    norm_total = lax.psum(jnp.sum(right_part * right_part), "mp")
    spectral = jnp.sqrt(norm_total + tiny_eps)
    return (spectral, right_part / spectral)


def on_device(features, labels, weights, vectors, head_weight):
    weight = weights[0]
    vector_u = vectors[0]
    micro_count, batch_rows, local_cols = features.shape
    full_width = weight.shape[0]
    sections = lax.axis_size("section")
    section_index = lax.axis_index("section")
    tick_count = micro_count + sections - 1
    sign_all = (2 * labels - 1).astype(jnp.float32)
    spectral_init, new_init = power_step(weight, vector_u)

    def forward_tick(tick_now, state_all):
        incoming, inputs_all, pre_all, logits_all, spectral, new_u = state_all
        micro_index = tick_now - section_index
        is_live = (micro_index >= 0) & (micro_index < micro_count)
        micro_slot = jnp.clip(micro_index, 0, micro_count - 1)
        first_input = lax.dynamic_index_in_dim(features, micro_slot, 0, keepdims=False)
        layer_in = jnp.where(section_index == 0, first_input, incoming)
        shard_piece = lax.all_gather(layer_in, "mp", axis=1, tiled=True)
        accum_part = jnp.dot(shard_piece, weight, preferred_element_type=jnp.float32)
        whole_rows = shard_piece
        accum_part, whole_rows = (accum_part, whole_rows)
        pre_act = accum_part / spectral
        layer_out = (layer_in.astype(jnp.float32) + jax.nn.silu(pre_act)).astype(jnp.bfloat16)
        partial_logit = jnp.sum(layer_out.astype(jnp.float32) * head_weight[None, :], axis=1)
        inputs_all = keep_slot(inputs_all, whole_rows, micro_slot, is_live)
        pre_all = keep_slot(pre_all, pre_act, micro_slot, is_live)
        logits_all = keep_slot(
            logits_all, partial_logit, micro_slot, is_live & (section_index == sections - 1)
        )
        incoming = shifted(layer_out, "section", 1)
        return (incoming, inputs_all, pre_all, logits_all, spectral, new_u)

    start_state = (
        jnp.zeros((batch_rows, local_cols), jnp.bfloat16),
        jnp.zeros((micro_count, batch_rows, full_width), jnp.bfloat16),
        jnp.zeros((micro_count, batch_rows, local_cols), jnp.float32),
        jnp.zeros((micro_count, batch_rows), jnp.float32),
        spectral_init,
        new_init,
    )
    _, inputs_all, pre_all, partial_logits, spectral, new_u = lax.fori_loop(
        0, tick_count, forward_tick, start_state
    )
    logits_all = lax.psum(partial_logits, "mp")

    def backward_tick(tick_now, state_all):
        incoming, grad_all = state_all
        micro_index = tick_now - (sections - 1 - section_index)
        is_live = (micro_index >= 0) & (micro_index < micro_count)
        micro_slot = jnp.clip(micro_index, 0, micro_count - 1)
        sign_row = lax.dynamic_index_in_dim(sign_all, micro_slot, 0, keepdims=False)
        logit_row = lax.dynamic_index_in_dim(logits_all, micro_slot, 0, keepdims=False)
        top_scale = -loss_scale * sign_row * jax.nn.sigmoid(-sign_row * logit_row)
        top_grad = (top_scale[:, None] * head_weight[None, :]).astype(jnp.bfloat16)
        grad_out = jnp.where(section_index == sections - 1, top_grad, incoming)
        pre_act = lax.dynamic_index_in_dim(pre_all, micro_slot, 0, keepdims=False)
        grad_pre = (grad_out.astype(jnp.float32) * silu_slope(pre_act)).astype(jnp.bfloat16)
        partial_term = lax.dot_general(
            grad_pre, weight, (((1,), (1,)), ((), ())), preferred_element_type=jnp.float32
        )
        received = lax.all_to_all(
            partial_term.astype(jnp.bfloat16), "mp", split_axis=1, concat_axis=0, tiled=True
        ).astype(partial_term.dtype)
        back_sum = jnp.sum(received.reshape(-1, batch_rows, local_cols), axis=0)
        grad_in = (grad_out.astype(jnp.float32) + back_sum / spectral).astype(jnp.bfloat16)
        grad_all = keep_slot(grad_all, grad_pre, micro_slot, is_live)
        incoming = shifted(grad_in, "section", -1)
        return (incoming, grad_all)

    back_state = (
        jnp.zeros((batch_rows, local_cols), jnp.bfloat16),
        jnp.zeros((micro_count, batch_rows, local_cols), jnp.bfloat16),
    )
    _, grad_all = lax.fori_loop(0, tick_count, backward_tick, back_state)
    whole_rows = inputs_all.reshape(micro_count * batch_rows, full_width)
    grad_rows = grad_all.reshape(micro_count * batch_rows, local_cols)
    outer_sum = lax.dot_general(
        whole_rows, grad_rows, (((0,), (0,)), ((), ())), preferred_element_type=jnp.float32
    )
    weight_grad = (outer_sum / spectral).astype(jnp.bfloat16)
    inner_total = lax.psum(jnp.sum(outer_sum * weight.astype(jnp.float32)), "mp")
    rank_coef = inner_total / (spectral * spectral)
    return (weight_grad[None], new_u[None], rank_coef.reshape(1))


def solution(mesh):
    placed = (P(None, None, "mp"), P(), P("section", None, "mp"), P("section", "mp"), P("mp"))
    return jax.shard_map(
        on_device,
        mesh=mesh,
        in_specs=placed,
        out_specs=(P("section", None, "mp"), P("section", "mp"), P("section")),
        check_vma=False,
    )
```

profile of v0, /device:TPU:0, one launch (start us, length us, event | category | flops | bytes accessed | tf_op | source)
XLA Modules:
  0.0 495.4 jit_solution(9324954132209440340)
XLA Ops:
  0.6 5.6 %fusion.15 = f32[1,8192]{1,0:T(1,128)S(1)} fusion(f32[1,512]{1,0:T(1,128)} %param.12, bf16[1,8192,512]{2,1,0:T(8,128)(2,1)} %param.11), kind=kOutput, calls=%fused_computation.44 | convolution fusion | flops 8389120 | bytes 8423424 | tf_op jit(solution)/shard_map/dot_general | solution.py:30
  6.3 63.0 %psum.28 = f32[8192]{0:T(1024)S(1)} all-reduce(f32[8192]{0:T(1024)S(1)} %bitcast.113), channel_id=1, replica_groups=mesh['section'=2,'mp'=16] {'mp'}, use_global_device_ids=true, to_apply=%region_0.0 | all-reduce | flops 8192 | bytes 65536 | tf_op jit(solution)/shard_map/psum | solution.py:30
  70.6 4.6 fusion.18
  75.8 30.1 %psum.29 = f32[]{:T(128)} all-reduce(f32[]{:T(128)} %multiply_reduce_fusion.2), channel_id=1, replica_groups=mesh['section'=2,'mp'=16] {'mp'}, use_global_device_ids=true, to_apply=%region_3.0 | all-reduce | flops 1 | bytes 8 | tf_op jit(solution)/shard_map/psum | solution.py:33
  107.4 158.8 %while.37 = (s32[]{:T(128)}, bf16[32,512]{1,0:T(8,128)(2,1)}, bf16[4,32,8192]{2,1,0:T(8,128)(2,1)S(1)}, f32[4,32,512]{2,1,0:T(8,128)S(1)}, f32[4,32]{1,0:T(4,128...) while((s32[]{:T(128)}, bf16[32,512]{1,0:T(8,128)(2,1)}, ...), condition=%wide.region_6.7_spmd, body=%wide.region_4.6_spmd.sunk | while | flops 268910592 | bytes 12782621 | solution.py:79
  108.2 18.7 %all_gather.9 = bf16[32,8192]{1,0:T(8,128)(2,1)S(1)} all-gather(bf16[32,512]{1,0:T(8,128)(2,1)S(1)} %bitcast_select_fusion.5), channel_id=1, replica_groups=mesh['section'=2,'mp'=16] {'mp'}, dimensions={1}, use_global_device_ids=true | all-gather | bytes 557056 | tf_op jit(solution)/shard_map/while/body/eval_jaxpr/all_gather | solution.py:56
  126.9 5.7 %multiply_reduce_fusion.4 = (f32[32]{0:T(128)S(1)}, bf16[32,512]{1,0:T(8,128)(2,1)}, f32[32,512]{1,0:T(8,128)S(1)}) fusion(f32[512]{0:T(512)S(1)} %get-tuple-element.704, bf16[32,512]{1,0:T(8,128)(2,1)S(1)} %bitcast_select_fusion.5, f32[]{:T(128)} %get-tuple-element.702, bf16[32,8192]{1,0:T(8,128)(2,1)S(1)} %all_gather.9, ...), kind=kOutput, calls=%fused_computation.5.clone.1 | convolution fusion | flops 268615648 | bytes 9046148 | tf_op jit(solution)/shard_map/while/body/eval_jaxpr/dot_general | solution.py:57
  132.5 4.0 collective-permute-start
  138.6 20.4 %all_gather.9 = bf16[32,8192]{1,0:T(8,128)(2,1)S(1)} all-gather(bf16[32,512]{1,0:T(8,128)(2,1)S(1)} %bitcast_select_fusion.5), channel_id=1, replica_groups=mesh['section'=2,'mp'=16] {'mp'}, dimensions={1}, use_global_device_ids=true | all-gather | bytes 557056 | tf_op jit(solution)/shard_map/while/body/eval_jaxpr/all_gather | solution.py:56
  159.1 5.7 %multiply_reduce_fusion.4 = (f32[32]{0:T(128)S(1)}, bf16[32,512]{1,0:T(8,128)(2,1)}, f32[32,512]{1,0:T(8,128)S(1)}) fusion(f32[512]{0:T(512)S(1)} %get-tuple-element.704, bf16[32,512]{1,0:T(8,128)(2,1)S(1)} %bitcast_select_fusion.5, f32[]{:T(128)} %get-tuple-element.702, bf16[32,8192]{1,0:T(8,128)(2,1)S(1)} %all_gather.9, ...), kind=kOutput, calls=%fused_computation.5.clone.1 | convolution fusion | flops 268615648 | bytes 9046148 | tf_op jit(solution)/shard_map/while/body/eval_jaxpr/dot_general | solution.py:57
  164.7 4.8 collective-permute-start
  171.6 18.7 %all_gather.9 = bf16[32,8192]{1,0:T(8,128)(2,1)S(1)} all-gather(bf16[32,512]{1,0:T(8,128)(2,1)S(1)} %bitcast_select_fusion.5), channel_id=1, replica_groups=mesh['section'=2,'mp'=16] {'mp'}, dimensions={1}, use_global_device_ids=true | all-gather | bytes 557056 | tf_op jit(solution)/shard_map/while/body/eval_jaxpr/all_gather | solution.py:56
  190.3 5.7 %multiply_reduce_fusion.4 = (f32[32]{0:T(128)S(1)}, bf16[32,512]{1,0:T(8,128)(2,1)}, f32[32,512]{1,0:T(8,128)S(1)}) fusion(f32[512]{0:T(512)S(1)} %get-tuple-element.704, bf16[32,512]{1,0:T(8,128)(2,1)S(1)} %bitcast_select_fusion.5, f32[]{:T(128)} %get-tuple-element.702, bf16[32,8192]{1,0:T(8,128)(2,1)S(1)} %all_gather.9, ...), kind=kOutput, calls=%fused_computation.5.clone.1 | convolution fusion | flops 268615648 | bytes 9046148 | tf_op jit(solution)/shard_map/while/body/eval_jaxpr/dot_general | solution.py:57
  195.9 4.8 collective-permute-start
  202.8 20.4 %all_gather.9 = bf16[32,8192]{1,0:T(8,128)(2,1)S(1)} all-gather(bf16[32,512]{1,0:T(8,128)(2,1)S(1)} %bitcast_select_fusion.5), channel_id=1, replica_groups=mesh['section'=2,'mp'=16] {'mp'}, dimensions={1}, use_global_device_ids=true | all-gather | bytes 557056 | tf_op jit(solution)/shard_map/while/body/eval_jaxpr/all_gather | solution.py:56
  223.3 5.7 %multiply_reduce_fusion.4 = (f32[32]{0:T(128)S(1)}, bf16[32,512]{1,0:T(8,128)(2,1)}, f32[32,512]{1,0:T(8,128)S(1)}) fusion(f32[512]{0:T(512)S(1)} %get-tuple-element.704, bf16[32,512]{1,0:T(8,128)(2,1)S(1)} %bitcast_select_fusion.5, f32[]{:T(128)} %get-tuple-element.702, bf16[32,8192]{1,0:T(8,128)(2,1)S(1)} %all_gather.9, ...), kind=kOutput, calls=%fused_computation.5.clone.1 | convolution fusion | flops 268615648 | bytes 9046148 | tf_op jit(solution)/shard_map/while/body/eval_jaxpr/dot_general | solution.py:57
  228.9 4.8 collective-permute-start
  235.8 18.7 %all_gather.9 = bf16[32,8192]{1,0:T(8,128)(2,1)S(1)} all-gather(bf16[32,512]{1,0:T(8,128)(2,1)S(1)} %bitcast_select_fusion.5), channel_id=1, replica_groups=mesh['section'=2,'mp'=16] {'mp'}, dimensions={1}, use_global_device_ids=true | all-gather | bytes 557056 | tf_op jit(solution)/shard_map/while/body/eval_jaxpr/all_gather | solution.py:56
  254.5 5.7 %multiply_reduce_fusion.4 = (f32[32]{0:T(128)S(1)}, bf16[32,512]{1,0:T(8,128)(2,1)}, f32[32,512]{1,0:T(8,128)S(1)}) fusion(f32[512]{0:T(512)S(1)} %get-tuple-element.704, bf16[32,512]{1,0:T(8,128)(2,1)S(1)} %bitcast_select_fusion.5, f32[]{:T(128)} %get-tuple-element.702, bf16[32,8192]{1,0:T(8,128)(2,1)S(1)} %all_gather.9, ...), kind=kOutput, calls=%fused_computation.5.clone.1 | convolution fusion | flops 268615648 | bytes 9046148 | tf_op jit(solution)/shard_map/while/body/eval_jaxpr/dot_general | solution.py:57
  260.1 4.8 collective-permute-start
  266.2 30.4 %psum.30 = f32[4,32]{1,0:T(4,128)S(1)} all-reduce(f32[4,32]{1,0:T(4,128)S(1)} %get-tuple-element.461), channel_id=1, replica_groups=mesh['section'=2,'mp'=16] {'mp'}, use_global_device_ids=true, to_apply=%region_7.8 | all-reduce | flops 128 | bytes 1024 | tf_op jit(solution)/shard_map/psum | solution.py:82
  297.4 155.4 %while.38 = (s32[]{:T(128)}, bf16[32,512]{1,0:T(8,128)(2,1)S(1)}, bf16[4,32,512]{2,1,0:T(8,128)(2,1)S(1)}, pred[]{:T(512)}, s32[]{:T(128)}, /*index=5*/f32[4,32]...) while((s32[]{:T(128)}, bf16[32,512]{1,0:T(8,128)(2,1)S(1)}, ...), condition=%wide.region_10.11_spmd, body=%wide.region_8.10_spmd.sunk | while | flops 269762784 | bytes 12787494 | solution.py:112
  297.4 5.9 %convolution_convert_fusion.2 = bf16[32,8192]{1,0:T(8,128)(2,1)S(1)} fusion(bf16[8192,512]{1,0:T(8,128)(2,1)} %get-tuple-element.748, f32[4,32,512]{2,1,0:T(8,128)S(1)} %get-tuple-element.747, s32[]{:T(128)S(6)} %min.21, bf16[32,512]{1,0:T(8,128)(2,1)S(1)} %get-tuple-element.725, f32[512]{0:T(512)S(1)} %get-tuple-element.746, f32[32]{0:T(128)S(1)} %fusion.37, ...), kind=kOutput, calls=%fused_computation.12.clone.1 | convolution fusion | flops 268910592 | bytes 9013765 | tf_op jit(solution)/shard_map/while/body/eval_jaxpr/dot_general | solution.py:96
  304.2 3.6 all-to-all-start
  307.8 14.2 %all-to-all-done = bf16[32,16,512]{2,0,1:T(8,128)(2,1)S(1)} async-done(((bf16[32,16,512]{2,0,1:T(8,128)(2,1)}), bf16[32,16,512]{2,0,1:T(8,128)(2,1)S(1)}, u32[]{:S(2)}, u32[]{:S(2)}) %all-to-all-start) | async-done | bytes 524320 | tf_op jit(solution)/shard_map/while/body/eval_jaxpr/all_to_all | solution.py:99
  322.2 1.3 collective-permute-start.1
  323.6 4.4 collective-permute-done.1
  328.0 5.9 %convolution_convert_fusion.2 = bf16[32,8192]{1,0:T(8,128)(2,1)S(1)} fusion(bf16[8192,512]{1,0:T(8,128)(2,1)} %get-tuple-element.748, f32[4,32,512]{2,1,0:T(8,128)S(1)} %get-tuple-element.747, s32[]{:T(128)S(6)} %min.21, bf16[32,512]{1,0:T(8,128)(2,1)S(1)} %get-tuple-element.725, f32[512]{0:T(512)S(1)} %get-tuple-element.746, f32[32]{0:T(128)S(1)} %fusion.37, ...), kind=kOutput, calls=%fused_computation.12.clone.1 | convolution fusion | flops 268910592 | bytes 9013765 | tf_op jit(solution)/shard_map/while/body/eval_jaxpr/dot_general | solution.py:96
  334.8 4.1 all-to-all-start
  338.9 14.2 %all-to-all-done = bf16[32,16,512]{2,0,1:T(8,128)(2,1)S(1)} async-done(((bf16[32,16,512]{2,0,1:T(8,128)(2,1)}), bf16[32,16,512]{2,0,1:T(8,128)(2,1)S(1)}, u32[]{:S(2)}, u32[]{:S(2)}) %all-to-all-start) | async-done | bytes 524320 | tf_op jit(solution)/shard_map/while/body/eval_jaxpr/all_to_all | solution.py:99
  353.3 1.3 collective-permute-start.1
  354.7 4.4 collective-permute-done.1
  359.1 5.9 %convolution_convert_fusion.2 = bf16[32,8192]{1,0:T(8,128)(2,1)S(1)} fusion(bf16[8192,512]{1,0:T(8,128)(2,1)} %get-tuple-element.748, f32[4,32,512]{2,1,0:T(8,128)S(1)} %get-tuple-element.747, s32[]{:T(128)S(6)} %min.21, bf16[32,512]{1,0:T(8,128)(2,1)S(1)} %get-tuple-element.725, f32[512]{0:T(512)S(1)} %get-tuple-element.746, f32[32]{0:T(128)S(1)} %fusion.37, ...), kind=kOutput, calls=%fused_computation.12.clone.1 | convolution fusion | flops 268910592 | bytes 9013765 | tf_op jit(solution)/shard_map/while/body/eval_jaxpr/dot_general | solution.py:96
  365.9 4.2 all-to-all-start
  370.1 14.2 %all-to-all-done = bf16[32,16,512]{2,0,1:T(8,128)(2,1)S(1)} async-done(((bf16[32,16,512]{2,0,1:T(8,128)(2,1)}), bf16[32,16,512]{2,0,1:T(8,128)(2,1)S(1)}, u32[]{:S(2)}, u32[]{:S(2)}) %all-to-all-start) | async-done | bytes 524320 | tf_op jit(solution)/shard_map/while/body/eval_jaxpr/all_to_all | solution.py:99
  384.5 1.3 collective-permute-start.1
  385.9 4.4 collective-permute-done.1
  390.4 5.9 %convolution_convert_fusion.2 = bf16[32,8192]{1,0:T(8,128)(2,1)S(1)} fusion(bf16[8192,512]{1,0:T(8,128)(2,1)} %get-tuple-element.748, f32[4,32,512]{2,1,0:T(8,128)S(1)} %get-tuple-element.747, s32[]{:T(128)S(6)} %min.21, bf16[32,512]{1,0:T(8,128)(2,1)S(1)} %get-tuple-element.725, f32[512]{0:T(512)S(1)} %get-tuple-element.746, f32[32]{0:T(128)S(1)} %fusion.37, ...), kind=kOutput, calls=%fused_computation.12.clone.1 | convolution fusion | flops 268910592 | bytes 9013765 | tf_op jit(solution)/shard_map/while/body/eval_jaxpr/dot_general | solution.py:96
  397.2 4.2 all-to-all-start
  401.3 14.2 %all-to-all-done = bf16[32,16,512]{2,0,1:T(8,128)(2,1)S(1)} async-done(((bf16[32,16,512]{2,0,1:T(8,128)(2,1)}), bf16[32,16,512]{2,0,1:T(8,128)(2,1)S(1)}, u32[]{:S(2)}, u32[]{:S(2)}) %all-to-all-start) | async-done | bytes 524320 | tf_op jit(solution)/shard_map/while/body/eval_jaxpr/all_to_all | solution.py:99
  415.8 1.3 collective-permute-start.1
  417.2 4.4 collective-permute-done.1
  421.6 5.9 %convolution_convert_fusion.2 = bf16[32,8192]{1,0:T(8,128)(2,1)S(1)} fusion(bf16[8192,512]{1,0:T(8,128)(2,1)} %get-tuple-element.748, f32[4,32,512]{2,1,0:T(8,128)S(1)} %get-tuple-element.747, s32[]{:T(128)S(6)} %min.21, bf16[32,512]{1,0:T(8,128)(2,1)S(1)} %get-tuple-element.725, f32[512]{0:T(512)S(1)} %get-tuple-element.746, f32[32]{0:T(128)S(1)} %fusion.37, ...), kind=kOutput, calls=%fused_computation.12.clone.1 | convolution fusion | flops 268910592 | bytes 9013765 | tf_op jit(solution)/shard_map/while/body/eval_jaxpr/dot_general | solution.py:96
  428.4 4.2 all-to-all-start
  432.6 14.2 %all-to-all-done = bf16[32,16,512]{2,0,1:T(8,128)(2,1)S(1)} async-done(((bf16[32,16,512]{2,0,1:T(8,128)(2,1)}), bf16[32,16,512]{2,0,1:T(8,128)(2,1)S(1)}, u32[]{:S(2)}, u32[]{:S(2)}) %all-to-all-start) | async-done | bytes 524320 | tf_op jit(solution)/shard_map/while/body/eval_jaxpr/all_to_all | solution.py:99
  448.4 4.4 collective-permute-done.1
  452.8 8.5 %fusion.13 = (f32[]{:T(128)}, bf16[1,8192,512]{2,1,0:T(8,128)(2,1)}) fusion(bf16[1,8192,512]{2,1,0:T(8,128)(2,1)} %bitcast.111, f32[]{:T(128)} %sqrt.3, bf16[4,32,8192]{2,1,0:T(8,128)(2,1)S(1)} %get-tuple-element.460, bf16[4,32,512]{2,1,0:T(8,128)(2,1)S(1)} %get-tuple-element.463), kind=kOutput, calls=%fused_computation.40 | convolution fusion | flops 1094713344 | bytes 19005448 | tf_op jit(solution)/shard_map/dot_general | solution.py:115
  461.3 31.7 %psum.31 = f32[]{:T(128)} all-reduce(f32[]{:T(128)} %get-tuple-element.513), channel_id=1, replica_groups=mesh['section'=2,'mp'=16] {'mp'}, use_global_device_ids=true, to_apply=%region_12.13 | all-reduce | flops 1 | bytes 8 | tf_op jit(solution)/shard_map/psum | solution.py:119
  (90 shorter events, 20.5 us)
Async XLA Ops:
  70.6 36.8 %copy-start = (f32[512]{0:T(512)S(1)}, f32[512]{0:T(512)}, u32[]{:S(2)}) copy-start(f32[512]{0:T(512)} %param.13) | copy-start | bytes 6148
  132.5 5.3 %collective-permute-start = (bf16[32,512]{1,0:T(8,128)(2,1)}, bf16[32,512]{1,0:T(8,128)(2,1)}, u32[]{:S(2)}, u32[]{:S(2)}) collective-permute-start(bf16[32,512]{1,0:T(8,128)(2,1)} %get-tuple-element.647), channel_id=1, source_target_pairs={{0,16},{1,17},{2,18},{3,19},{4,20},{5,21},{6,22},{7,23},{8,24},{9,... | collective-permute-start | bytes 98312 | tf_op jit(solution)/shard_map/while/body/eval_jaxpr/ppermute | solution.py:13
  164.7 6.1 %collective-permute-start = (bf16[32,512]{1,0:T(8,128)(2,1)}, bf16[32,512]{1,0:T(8,128)(2,1)}, u32[]{:S(2)}, u32[]{:S(2)}) collective-permute-start(bf16[32,512]{1,0:T(8,128)(2,1)} %get-tuple-element.647), channel_id=1, source_target_pairs={{0,16},{1,17},{2,18},{3,19},{4,20},{5,21},{6,22},{7,23},{8,24},{9,... | collective-permute-start | bytes 98312 | tf_op jit(solution)/shard_map/while/body/eval_jaxpr/ppermute | solution.py:13
  195.9 6.1 %collective-permute-start = (bf16[32,512]{1,0:T(8,128)(2,1)}, bf16[32,512]{1,0:T(8,128)(2,1)}, u32[]{:S(2)}, u32[]{:S(2)}) collective-permute-start(bf16[32,512]{1,0:T(8,128)(2,1)} %get-tuple-element.647), channel_id=1, source_target_pairs={{0,16},{1,17},{2,18},{3,19},{4,20},{5,21},{6,22},{7,23},{8,24},{9,... | collective-permute-start | bytes 98312 | tf_op jit(solution)/shard_map/while/body/eval_jaxpr/ppermute | solution.py:13
  228.9 6.1 %collective-permute-start = (bf16[32,512]{1,0:T(8,128)(2,1)}, bf16[32,512]{1,0:T(8,128)(2,1)}, u32[]{:S(2)}, u32[]{:S(2)}) collective-permute-start(bf16[32,512]{1,0:T(8,128)(2,1)} %get-tuple-element.647), channel_id=1, source_target_pairs={{0,16},{1,17},{2,18},{3,19},{4,20},{5,21},{6,22},{7,23},{8,24},{9,... | collective-permute-start | bytes 98312 | tf_op jit(solution)/shard_map/while/body/eval_jaxpr/ppermute | solution.py:13
  260.1 6.1 %collective-permute-start = (bf16[32,512]{1,0:T(8,128)(2,1)}, bf16[32,512]{1,0:T(8,128)(2,1)}, u32[]{:S(2)}, u32[]{:S(2)}) collective-permute-start(bf16[32,512]{1,0:T(8,128)(2,1)} %get-tuple-element.647), channel_id=1, source_target_pairs={{0,16},{1,17},{2,18},{3,19},{4,20},{5,21},{6,22},{7,23},{8,24},{9,... | collective-permute-start | bytes 98312 | tf_op jit(solution)/shard_map/while/body/eval_jaxpr/ppermute | solution.py:13
  304.2 17.8 %all-to-all-start = ((bf16[32,16,512]{2,0,1:T(8,128)(2,1)}), bf16[32,16,512]{2,0,1:T(8,128)(2,1)S(1)}, u32[]{:S(2)}, u32[]{:S(2)}) async-start(bf16[32,16,512]{2,0,1:T(8,128)(2,1)} %bitcast.109), calls=%async_computation | async-start | bytes 1048576 | tf_op jit(solution)/shard_map/while/body/eval_jaxpr/all_to_all | solution.py:99
  322.2 5.8 %collective-permute-start.1 = (bf16[32,512]{1,0:T(8,128)(2,1)S(1)}, bf16[32,512]{1,0:T(8,128)(2,1)S(1)}, u32[]{:S(2)}, u32[]{:S(2)}) collective-permute-start(bf16[32,512]{1,0:T(8,128)(2,1)S(1)} %fusion.38), channel_id=1, source_target_pairs={{16,0},{17,1},{18,2},{19,3},{20,4},{21,5},{22,6},{23,7},{24,8},{25... | collective-permute-start | bytes 98312 | tf_op jit(solution)/shard_map/while/body/eval_jaxpr/ppermute | solution.py:13
  334.8 18.4 %all-to-all-start = ((bf16[32,16,512]{2,0,1:T(8,128)(2,1)}), bf16[32,16,512]{2,0,1:T(8,128)(2,1)S(1)}, u32[]{:S(2)}, u32[]{:S(2)}) async-start(bf16[32,16,512]{2,0,1:T(8,128)(2,1)} %bitcast.109), calls=%async_computation | async-start | bytes 1048576 | tf_op jit(solution)/shard_map/while/body/eval_jaxpr/all_to_all | solution.py:99
  353.3 5.8 %collective-permute-start.1 = (bf16[32,512]{1,0:T(8,128)(2,1)S(1)}, bf16[32,512]{1,0:T(8,128)(2,1)S(1)}, u32[]{:S(2)}, u32[]{:S(2)}) collective-permute-start(bf16[32,512]{1,0:T(8,128)(2,1)S(1)} %fusion.38), channel_id=1, source_target_pairs={{16,0},{17,1},{18,2},{19,3},{20,4},{21,5},{22,6},{23,7},{24,8},{25... | collective-permute-start | bytes 98312 | tf_op jit(solution)/shard_map/while/body/eval_jaxpr/ppermute | solution.py:13
  365.9 18.4 %all-to-all-start = ((bf16[32,16,512]{2,0,1:T(8,128)(2,1)}), bf16[32,16,512]{2,0,1:T(8,128)(2,1)S(1)}, u32[]{:S(2)}, u32[]{:S(2)}) async-start(bf16[32,16,512]{2,0,1:T(8,128)(2,1)} %bitcast.109), calls=%async_computation | async-start | bytes 1048576 | tf_op jit(solution)/shard_map/while/body/eval_jaxpr/all_to_all | solution.py:99
  384.5 5.8 %collective-permute-start.1 = (bf16[32,512]{1,0:T(8,128)(2,1)S(1)}, bf16[32,512]{1,0:T(8,128)(2,1)S(1)}, u32[]{:S(2)}, u32[]{:S(2)}) collective-permute-start(bf16[32,512]{1,0:T(8,128)(2,1)S(1)} %fusion.38), channel_id=1, source_target_pairs={{16,0},{17,1},{18,2},{19,3},{20,4},{21,5},{22,6},{23,7},{24,8},{25... | collective-permute-start | bytes 98312 | tf_op jit(solution)/shard_map/while/body/eval_jaxpr/ppermute | solution.py:13
  397.2 18.4 %all-to-all-start = ((bf16[32,16,512]{2,0,1:T(8,128)(2,1)}), bf16[32,16,512]{2,0,1:T(8,128)(2,1)S(1)}, u32[]{:S(2)}, u32[]{:S(2)}) async-start(bf16[32,16,512]{2,0,1:T(8,128)(2,1)} %bitcast.109), calls=%async_computation | async-start | bytes 1048576 | tf_op jit(solution)/shard_map/while/body/eval_jaxpr/all_to_all | solution.py:99
  415.8 5.8 %collective-permute-start.1 = (bf16[32,512]{1,0:T(8,128)(2,1)S(1)}, bf16[32,512]{1,0:T(8,128)(2,1)S(1)}, u32[]{:S(2)}, u32[]{:S(2)}) collective-permute-start(bf16[32,512]{1,0:T(8,128)(2,1)S(1)} %fusion.38), channel_id=1, source_target_pairs={{16,0},{17,1},{18,2},{19,3},{20,4},{21,5},{22,6},{23,7},{24,8},{25... | collective-permute-start | bytes 98312 | tf_op jit(solution)/shard_map/while/body/eval_jaxpr/ppermute | solution.py:13
  428.4 18.4 %all-to-all-start = ((bf16[32,16,512]{2,0,1:T(8,128)(2,1)}), bf16[32,16,512]{2,0,1:T(8,128)(2,1)S(1)}, u32[]{:S(2)}, u32[]{:S(2)}) async-start(bf16[32,16,512]{2,0,1:T(8,128)(2,1)} %bitcast.109), calls=%async_computation | async-start | bytes 1048576 | tf_op jit(solution)/shard_map/while/body/eval_jaxpr/all_to_all | solution.py:99
  447.0 5.8 %collective-permute-start.1 = (bf16[32,512]{1,0:T(8,128)(2,1)S(1)}, bf16[32,512]{1,0:T(8,128)(2,1)S(1)}, u32[]{:S(2)}, u32[]{:S(2)}) collective-permute-start(bf16[32,512]{1,0:T(8,128)(2,1)S(1)} %fusion.38), channel_id=1, source_target_pairs={{16,0},{17,1},{18,2},{19,3},{20,4},{21,5},{22,6},{23,7},{24,8},{25... | collective-permute-start | bytes 98312 | tf_op jit(solution)/shard_map/while/body/eval_jaxpr/ppermute | solution.py:13
where the time goes:
time: 497 us; the launch traced here: 495 us
  blocking collectives  252 us (51%)
  waiting for transfers between devices  98.3 us (20%)
  matrix products  76.6 us (15%)
  starting transfers between devices  49.8 us (10%)
  other arithmetic  8.44 us (2%)
  local copies, waits for them, and re-layouts  5.69 us (1%)
    all_gather x5, blocking collectives, forward_tick(): shard_piece = lax.all_gather(layer_in, 'mp', axis=1, tiled=True)  97 us
    all_to_all x5, waiting for transfers between devices, backward_tick(): lax.all_to_all(partial_term.astype(jnp.bfloat16), 'mp', split_axis=1, con...  71.2 us
    psum x1, blocking collectives, power_step(): lax.psum(jnp.dot(weight, vector_bf, preferred_element_type=jnp.float32),...  63 us
    psum x1, blocking collectives, on_device(): lax.psum(jnp.sum(outer_sum * weight.astype(jnp.float32)), 'mp')  31.7 us
    psum x1, blocking collectives, on_device(): logits_all = lax.psum(partial_logits, 'mp')  30.4 us
    psum x1, blocking collectives, power_step(): norm_total = lax.psum(jnp.sum(right_part * right_part), 'mp')  30.1 us
    ppermute x10, starting transfers between devices, shifted(): return lax.ppermute(block, axis, route)  29.6 us
    dot_general x5, matrix products, backward_tick(): lax.dot_general(grad_pre, weight, (((1,), (1,)), ((), ())), preferred_ele...  29.6 us
  transfers between devices with their start and end apart: 15, of which 15 were waited for; matrix products, arithmetic and copies ran while one was open for 0% of the time, Pallas kernels for 0%

commit v1 on v0

--- a/solution.py
+++ b/solution.py
@@ -27,7 +27,9 @@
 
 def power_step(weight, vector_u):
     vector_bf = vector_u.astype(jnp.bfloat16)
-    left_sum = lax.psum(jnp.dot(weight, vector_bf, preferred_element_type=jnp.float32), "mp")
+    part = jnp.dot(weight, vector_bf, preferred_element_type=jnp.float32)
+    pieces = lax.all_gather(part, "mp")
+    left_sum = jnp.sum(pieces, axis=0)
     vector_v = (left_sum * lax.rsqrt(jnp.sum(left_sum * left_sum) + tiny_eps)).astype(jnp.bfloat16)
     right_part = jnp.dot(vector_v, weight, preferred_element_type=jnp.float32)
     norm_total = lax.psum(jnp.sum(right_part * right_part), "mp")

time: 497 us -> 459 us (0.924)
  blocking collectives: 252 us -> 214 us
    psum x1 -> x0, blocking collectives: 63 us -> none  [power_step(): lax.psum(jnp.dot(weight, vector_bf, preferred_element_type=jnp.float32),...]
    all_gather x0 -> x1, blocking collectives: none -> 24.6 us  [power_step(): pieces = lax.all_gather(part, 'mp')]
where the time goes in v1:
time: 459 us; the launch traced here: 458 us
  blocking collectives  214 us (47%)
  waiting for transfers between devices  98.3 us (21%)
  matrix products  76.6 us (17%)
  starting transfers between devices  49.8 us (11%)
  other arithmetic  8.52 us (2%)
  local copies, waits for them, and re-layouts  5.79 us (1%)
    all_gather x5, blocking collectives, forward_tick(): shard_piece = lax.all_gather(layer_in, 'mp', axis=1, tiled=True)  97 us
    all_to_all x5, waiting for transfers between devices, backward_tick(): lax.all_to_all(partial_term.astype(jnp.bfloat16), 'mp', split_axis=1, con...  71.2 us
    psum x1, blocking collectives, on_device(): lax.psum(jnp.sum(outer_sum * weight.astype(jnp.float32)), 'mp')  31.7 us
    psum x1, blocking collectives, power_step(): norm_total = lax.psum(jnp.sum(right_part * right_part), 'mp')  30.4 us
    psum x1, blocking collectives, on_device(): logits_all = lax.psum(partial_logits, 'mp')  30.3 us
    ppermute x10, starting transfers between devices, shifted(): return lax.ppermute(block, axis, route)  29.7 us
    dot_general x5, matrix products, backward_tick(): lax.dot_general(grad_pre, weight, (((1,), (1,)), ((), ())), preferred_ele...  29.6 us
    dot_general x5, matrix products, forward_tick(): jnp.dot(shard_piece, weight, preferred_element_type=jnp.float32)  28.3 us
  transfers between devices with their start and end apart: 15, of which 15 were waited for; matrix products, arithmetic and copies ran while one was open for 0% of the time, Pallas kernels for 0%

profile of v1, /device:TPU:0, one launch (start us, length us, event | category | flops | bytes accessed | tf_op | source)
XLA Modules:
  0.0 457.5 jit_solution(6151154486589037833)
XLA Ops:
  0.6 5.6 %fusion.15 = f32[1,8192]{1,0:T(1,128)S(1)} fusion(f32[1,512]{1,0:T(1,128)} %param.12, bf16[1,8192,512]{2,1,0:T(8,128)(2,1)} %param.11), kind=kOutput, calls=%fused_computation.44 | convolution fusion | flops 8389120 | bytes 8423424 | tf_op jit(solution)/shard_map/dot_general | solution.py:30
  6.3 24.6 %all-gather = f32[131072]{0:T(1024)S(1)} all-gather(f32[8192]{0:T(1024)S(1)} %bitcast.113), channel_id=2, replica_groups=mesh['section'=2,'mp'=16] {'mp'}, dimensions={0}, use_global_device_ids=true | all-gather | bytes 557056 | tf_op jit(solution)/shard_map/all_gather | solution.py:31
  32.4 4.6 fusion.18
  37.6 30.4 %psum.21 = f32[]{:T(128)} all-reduce(f32[]{:T(128)} %multiply_reduce_fusion.2), channel_id=1, replica_groups=mesh['section'=2,'mp'=16] {'mp'}, use_global_device_ids=true, to_apply=%region_3.0 | all-reduce | flops 1 | bytes 8 | tf_op jit(solution)/shard_map/psum | solution.py:35
  69.6 158.9 %while.37 = (s32[]{:T(128)}, bf16[32,512]{1,0:T(8,128)(2,1)}, bf16[4,32,8192]{2,1,0:T(8,128)(2,1)S(1)}, f32[4,32,512]{2,1,0:T(8,128)S(1)}, f32[4,32]{1,0:T(4,128...) while((s32[]{:T(128)}, bf16[32,512]{1,0:T(8,128)(2,1)}, ...), condition=%wide.region_6.7_spmd, body=%wide.region_4.6_spmd.sunk | while | flops 268910592 | bytes 12782621 | solution.py:81
  70.4 18.8 %all_gather.17 = bf16[32,8192]{1,0:T(8,128)(2,1)S(1)} all-gather(bf16[32,512]{1,0:T(8,128)(2,1)S(1)} %bitcast_select_fusion.5), channel_id=1, replica_groups=mesh['section'=2,'mp'=16] {'mp'}, dimensions={1}, use_global_device_ids=true | all-gather | bytes 557056 | tf_op jit(solution)/shard_map/while/body/eval_jaxpr/all_gather | solution.py:58
  89.1 5.7 %multiply_reduce_fusion.4 = (f32[32]{0:T(128)S(1)}, bf16[32,512]{1,0:T(8,128)(2,1)}, f32[32,512]{1,0:T(8,128)S(1)}) fusion(f32[512]{0:T(512)S(1)} %get-tuple-element.704, bf16[32,512]{1,0:T(8,128)(2,1)S(1)} %bitcast_select_fusion.5, f32[]{:T(128)} %get-tuple-element.702, bf16[32,8192]{1,0:T(8,128)(2,1)S(1)} %all_gather.17, ...), kind=kOutput, calls=%fused_computation.5.clone.1 | convolution fusion | flops 268615648 | bytes 9046148 | tf_op jit(solution)/shard_map/while/body/eval_jaxpr/dot_general | solution.py:59
  94.8 4.0 collective-permute-start
  100.9 20.4 %all_gather.17 = bf16[32,8192]{1,0:T(8,128)(2,1)S(1)} all-gather(bf16[32,512]{1,0:T(8,128)(2,1)S(1)} %bitcast_select_fusion.5), channel_id=1, replica_groups=mesh['section'=2,'mp'=16] {'mp'}, dimensions={1}, use_global_device_ids=true | all-gather | bytes 557056 | tf_op jit(solution)/shard_map/while/body/eval_jaxpr/all_gather | solution.py:58
  121.3 5.7 %multiply_reduce_fusion.4 = (f32[32]{0:T(128)S(1)}, bf16[32,512]{1,0:T(8,128)(2,1)}, f32[32,512]{1,0:T(8,128)S(1)}) fusion(f32[512]{0:T(512)S(1)} %get-tuple-element.704, bf16[32,512]{1,0:T(8,128)(2,1)S(1)} %bitcast_select_fusion.5, f32[]{:T(128)} %get-tuple-element.702, bf16[32,8192]{1,0:T(8,128)(2,1)S(1)} %all_gather.17, ...), kind=kOutput, calls=%fused_computation.5.clone.1 | convolution fusion | flops 268615648 | bytes 9046148 | tf_op jit(solution)/shard_map/while/body/eval_jaxpr/dot_general | solution.py:59
  126.9 4.7 %collective-permute-start = (bf16[32,512]{1,0:T(8,128)(2,1)}, bf16[32,512]{1,0:T(8,128)(2,1)}, u32[]{:S(2)}, u32[]{:S(2)}) collective-permute-start(bf16[32,512]{1,0:T(8,128)(2,1)} %get-tuple-element.647), channel_id=1, source_target_pairs={{0,16},{1,17},{2,18},{3,19},{4,20},{5,21},{6,22},{7,23},{8,24},{9,... | collective-permute-start | bytes 98312 | tf_op jit(solution)/shard_map/while/body/eval_jaxpr/ppermute | solution.py:13
  133.7 18.8 %all_gather.17 = bf16[32,8192]{1,0:T(8,128)(2,1)S(1)} all-gather(bf16[32,512]{1,0:T(8,128)(2,1)S(1)} %bitcast_select_fusion.5), channel_id=1, replica_groups=mesh['section'=2,'mp'=16] {'mp'}, dimensions={1}, use_global_device_ids=true | all-gather | bytes 557056 | tf_op jit(solution)/shard_map/while/body/eval_jaxpr/all_gather | solution.py:58
  152.5 5.7 %multiply_reduce_fusion.4 = (f32[32]{0:T(128)S(1)}, bf16[32,512]{1,0:T(8,128)(2,1)}, f32[32,512]{1,0:T(8,128)S(1)}) fusion(f32[512]{0:T(512)S(1)} %get-tuple-element.704, bf16[32,512]{1,0:T(8,128)(2,1)S(1)} %bitcast_select_fusion.5, f32[]{:T(128)} %get-tuple-element.702, bf16[32,8192]{1,0:T(8,128)(2,1)S(1)} %all_gather.17, ...), kind=kOutput, calls=%fused_computation.5.clone.1 | convolution fusion | flops 268615648 | bytes 9046148 | tf_op jit(solution)/shard_map/while/body/eval_jaxpr/dot_general | solution.py:59
  158.2 4.8 %collective-permute-start = (bf16[32,512]{1,0:T(8,128)(2,1)}, bf16[32,512]{1,0:T(8,128)(2,1)}, u32[]{:S(2)}, u32[]{:S(2)}) collective-permute-start(bf16[32,512]{1,0:T(8,128)(2,1)} %get-tuple-element.647), channel_id=1, source_target_pairs={{0,16},{1,17},{2,18},{3,19},{4,20},{5,21},{6,22},{7,23},{8,24},{9,... | collective-permute-start | bytes 98312 | tf_op jit(solution)/shard_map/while/body/eval_jaxpr/ppermute | solution.py:13
  165.1 20.4 %all_gather.17 = bf16[32,8192]{1,0:T(8,128)(2,1)S(1)} all-gather(bf16[32,512]{1,0:T(8,128)(2,1)S(1)} %bitcast_select_fusion.5), channel_id=1, replica_groups=mesh['section'=2,'mp'=16] {'mp'}, dimensions={1}, use_global_device_ids=true | all-gather | bytes 557056 | tf_op jit(solution)/shard_map/while/body/eval_jaxpr/all_gather | solution.py:58
  185.4 5.7 %multiply_reduce_fusion.4 = (f32[32]{0:T(128)S(1)}, bf16[32,512]{1,0:T(8,128)(2,1)}, f32[32,512]{1,0:T(8,128)S(1)}) fusion(f32[512]{0:T(512)S(1)} %get-tuple-element.704, bf16[32,512]{1,0:T(8,128)(2,1)S(1)} %bitcast_select_fusion.5, f32[]{:T(128)} %get-tuple-element.702, bf16[32,8192]{1,0:T(8,128)(2,1)S(1)} %all_gather.17, ...), kind=kOutput, calls=%fused_computation.5.clone.1 | convolution fusion | flops 268615648 | bytes 9046148 | tf_op jit(solution)/shard_map/while/body/eval_jaxpr/dot_general | solution.py:59
  191.1 4.7 %collective-permute-start = (bf16[32,512]{1,0:T(8,128)(2,1)}, bf16[32,512]{1,0:T(8,128)(2,1)}, u32[]{:S(2)}, u32[]{:S(2)}) collective-permute-start(bf16[32,512]{1,0:T(8,128)(2,1)} %get-tuple-element.647), channel_id=1, source_target_pairs={{0,16},{1,17},{2,18},{3,19},{4,20},{5,21},{6,22},{7,23},{8,24},{9,... | collective-permute-start | bytes 98312 | tf_op jit(solution)/shard_map/while/body/eval_jaxpr/ppermute | solution.py:13
  197.9 18.8 %all_gather.17 = bf16[32,8192]{1,0:T(8,128)(2,1)S(1)} all-gather(bf16[32,512]{1,0:T(8,128)(2,1)S(1)} %bitcast_select_fusion.5), channel_id=1, replica_groups=mesh['section'=2,'mp'=16] {'mp'}, dimensions={1}, use_global_device_ids=true | all-gather | bytes 557056 | tf_op jit(solution)/shard_map/while/body/eval_jaxpr/all_gather | solution.py:58
  216.7 5.7 %multiply_reduce_fusion.4 = (f32[32]{0:T(128)S(1)}, bf16[32,512]{1,0:T(8,128)(2,1)}, f32[32,512]{1,0:T(8,128)S(1)}) fusion(f32[512]{0:T(512)S(1)} %get-tuple-element.704, bf16[32,512]{1,0:T(8,128)(2,1)S(1)} %bitcast_select_fusion.5, f32[]{:T(128)} %get-tuple-element.702, bf16[32,8192]{1,0:T(8,128)(2,1)S(1)} %all_gather.17, ...), kind=kOutput, calls=%fused_computation.5.clone.1 | convolution fusion | flops 268615648 | bytes 9046148 | tf_op jit(solution)/shard_map/while/body/eval_jaxpr/dot_general | solution.py:59
  222.3 4.8 %collective-permute-start = (bf16[32,512]{1,0:T(8,128)(2,1)}, bf16[32,512]{1,0:T(8,128)(2,1)}, u32[]{:S(2)}, u32[]{:S(2)}) collective-permute-start(bf16[32,512]{1,0:T(8,128)(2,1)} %get-tuple-element.647), channel_id=1, source_target_pairs={{0,16},{1,17},{2,18},{3,19},{4,20},{5,21},{6,22},{7,23},{8,24},{9,... | collective-permute-start | bytes 98312 | tf_op jit(solution)/shard_map/while/body/eval_jaxpr/ppermute | solution.py:13
  228.5 30.3 %psum.22 = f32[4,32]{1,0:T(4,128)S(1)} all-reduce(f32[4,32]{1,0:T(4,128)S(1)} %get-tuple-element.461), channel_id=1, replica_groups=mesh['section'=2,'mp'=16] {'mp'}, use_global_device_ids=true, to_apply=%region_7.8 | all-reduce | flops 128 | bytes 1024 | tf_op jit(solution)/shard_map/psum | solution.py:84
  259.5 155.4 %while.38 = (s32[]{:T(128)}, bf16[32,512]{1,0:T(8,128)(2,1)S(1)}, bf16[4,32,512]{2,1,0:T(8,128)(2,1)S(1)}, pred[]{:T(512)}, s32[]{:T(128)}, /*index=5*/f32[4,32]...) while((s32[]{:T(128)}, bf16[32,512]{1,0:T(8,128)(2,1)S(1)}, ...), condition=%wide.region_10.11_spmd, body=%wide.region_8.10_spmd.sunk | while | flops 269762784 | bytes 12787494 | solution.py:114
  259.6 5.9 %convolution_convert_fusion.2 = bf16[32,8192]{1,0:T(8,128)(2,1)S(1)} fusion(bf16[8192,512]{1,0:T(8,128)(2,1)} %get-tuple-element.748, f32[4,32,512]{2,1,0:T(8,128)S(1)} %get-tuple-element.747, s32[]{:T(128)S(6)} %min.21, bf16[32,512]{1,0:T(8,128)(2,1)S(1)} %get-tuple-element.725, f32[512]{0:T(512)S(1)} %get-tuple-element.746, f32[32]{0:T(128)S(1)} %fusion.37, ...), kind=kOutput, calls=%fused_computation.12.clone.1 | convolution fusion | flops 268910592 | bytes 9013765 | tf_op jit(solution)/shard_map/while/body/eval_jaxpr/dot_general | solution.py:98
  266.3 3.6 all-to-all-start
  270.0 14.2 %all-to-all-done = bf16[32,16,512]{2,0,1:T(8,128)(2,1)S(1)} async-done(((bf16[32,16,512]{2,0,1:T(8,128)(2,1)}), bf16[32,16,512]{2,0,1:T(8,128)(2,1)S(1)}, u32[]{:S(2)}, u32[]{:S(2)}) %all-to-all-start) | async-done | bytes 524320 | tf_op jit(solution)/shard_map/while/body/eval_jaxpr/all_to_all | solution.py:101
  284.3 1.3 collective-permute-start.1
  285.7 4.4 collective-permute-done.1
  290.1 5.9 %convolution_convert_fusion.2 = bf16[32,8192]{1,0:T(8,128)(2,1)S(1)} fusion(bf16[8192,512]{1,0:T(8,128)(2,1)} %get-tuple-element.748, f32[4,32,512]{2,1,0:T(8,128)S(1)} %get-tuple-element.747, s32[]{:T(128)S(6)} %min.21, bf16[32,512]{1,0:T(8,128)(2,1)S(1)} %get-tuple-element.725, f32[512]{0:T(512)S(1)} %get-tuple-element.746, f32[32]{0:T(128)S(1)} %fusion.37, ...), kind=kOutput, calls=%fused_computation.12.clone.1 | convolution fusion | flops 268910592 | bytes 9013765 | tf_op jit(solution)/shard_map/while/body/eval_jaxpr/dot_general | solution.py:98
  296.9 4.1 all-to-all-start
  301.1 14.2 %all-to-all-done = bf16[32,16,512]{2,0,1:T(8,128)(2,1)S(1)} async-done(((bf16[32,16,512]{2,0,1:T(8,128)(2,1)}), bf16[32,16,512]{2,0,1:T(8,128)(2,1)S(1)}, u32[]{:S(2)}, u32[]{:S(2)}) %all-to-all-start) | async-done | bytes 524320 | tf_op jit(solution)/shard_map/while/body/eval_jaxpr/all_to_all | solution.py:101
  316.9 4.4 collective-permute-done.1
  321.3 5.9 %convolution_convert_fusion.2 = bf16[32,8192]{1,0:T(8,128)(2,1)S(1)} fusion(bf16[8192,512]{1,0:T(8,128)(2,1)} %get-tuple-element.748, f32[4,32,512]{2,1,0:T(8,128)S(1)} %get-tuple-element.747, s32[]{:T(128)S(6)} %min.21, bf16[32,512]{1,0:T(8,128)(2,1)S(1)} %get-tuple-element.725, f32[512]{0:T(512)S(1)} %get-tuple-element.746, f32[32]{0:T(128)S(1)} %fusion.37, ...), kind=kOutput, calls=%fused_computation.12.clone.1 | convolution fusion | flops 268910592 | bytes 9013765 | tf_op jit(solution)/shard_map/while/body/eval_jaxpr/dot_general | solution.py:98
  328.1 4.2 all-to-all-start
  332.3 14.2 %all-to-all-done = bf16[32,16,512]{2,0,1:T(8,128)(2,1)S(1)} async-done(((bf16[32,16,512]{2,0,1:T(8,128)(2,1)}), bf16[32,16,512]{2,0,1:T(8,128)(2,1)S(1)}, u32[]{:S(2)}, u32[]{:S(2)}) %all-to-all-start) | async-done | bytes 524320 | tf_op jit(solution)/shard_map/while/body/eval_jaxpr/all_to_all | solution.py:101
  346.7 1.3 collective-permute-start.1
  348.1 4.4 collective-permute-done.1
  352.5 5.9 %convolution_convert_fusion.2 = bf16[32,8192]{1,0:T(8,128)(2,1)S(1)} fusion(bf16[8192,512]{1,0:T(8,128)(2,1)} %get-tuple-element.748, f32[4,32,512]{2,1,0:T(8,128)S(1)} %get-tuple-element.747, s32[]{:T(128)S(6)} %min.21, bf16[32,512]{1,0:T(8,128)(2,1)S(1)} %get-tuple-element.725, f32[512]{0:T(512)S(1)} %get-tuple-element.746, f32[32]{0:T(128)S(1)} %fusion.37, ...), kind=kOutput, calls=%fused_computation.12.clone.1 | convolution fusion | flops 268910592 | bytes 9013765 | tf_op jit(solution)/shard_map/while/body/eval_jaxpr/dot_general | solution.py:98
  359.3 4.2 all-to-all-start
  363.5 14.2 %all-to-all-done = bf16[32,16,512]{2,0,1:T(8,128)(2,1)S(1)} async-done(((bf16[32,16,512]{2,0,1:T(8,128)(2,1)}), bf16[32,16,512]{2,0,1:T(8,128)(2,1)S(1)}, u32[]{:S(2)}, u32[]{:S(2)}) %all-to-all-start) | async-done | bytes 524320 | tf_op jit(solution)/shard_map/while/body/eval_jaxpr/all_to_all | solution.py:101
  377.9 1.3 collective-permute-start.1
  379.3 4.4 collective-permute-done.1
  383.7 5.9 %convolution_convert_fusion.2 = bf16[32,8192]{1,0:T(8,128)(2,1)S(1)} fusion(bf16[8192,512]{1,0:T(8,128)(2,1)} %get-tuple-element.748, f32[4,32,512]{2,1,0:T(8,128)S(1)} %get-tuple-element.747, s32[]{:T(128)S(6)} %min.21, bf16[32,512]{1,0:T(8,128)(2,1)S(1)} %get-tuple-element.725, f32[512]{0:T(512)S(1)} %get-tuple-element.746, f32[32]{0:T(128)S(1)} %fusion.37, ...), kind=kOutput, calls=%fused_computation.12.clone.1 | convolution fusion | flops 268910592 | bytes 9013765 | tf_op jit(solution)/shard_map/while/body/eval_jaxpr/dot_general | solution.py:98
  390.5 4.2 all-to-all-start
  394.7 14.2 %all-to-all-done = bf16[32,16,512]{2,0,1:T(8,128)(2,1)S(1)} async-done(((bf16[32,16,512]{2,0,1:T(8,128)(2,1)}), bf16[32,16,512]{2,0,1:T(8,128)(2,1)S(1)}, u32[]{:S(2)}, u32[]{:S(2)}) %all-to-all-start) | async-done | bytes 524320 | tf_op jit(solution)/shard_map/while/body/eval_jaxpr/all_to_all | solution.py:101
  409.1 1.3 collective-permute-start.1
  410.5 4.4 collective-permute-done.1
  414.9 8.5 %fusion.13 = (f32[]{:T(128)}, bf16[1,8192,512]{2,1,0:T(8,128)(2,1)}) fusion(bf16[1,8192,512]{2,1,0:T(8,128)(2,1)} %bitcast.111, f32[]{:T(128)} %sqrt.3, bf16[4,32,8192]{2,1,0:T(8,128)(2,1)S(1)} %get-tuple-element.460, bf16[4,32,512]{2,1,0:T(8,128)(2,1)S(1)} %get-tuple-element.463), kind=kOutput, calls=%fused_computation.40 | convolution fusion | flops 1094713344 | bytes 19005448 | tf_op jit(solution)/shard_map/dot_general | solution.py:117
  423.4 31.7 %psum.23 = f32[]{:T(128)} all-reduce(f32[]{:T(128)} %get-tuple-element.513), channel_id=1, replica_groups=mesh['section'=2,'mp'=16] {'mp'}, use_global_device_ids=true, to_apply=%region_12.13 | all-reduce | flops 1 | bytes 8 | tf_op jit(solution)/shard_map/psum | solution.py:121
  (92 shorter events, 20.6 us)
Async XLA Ops:
  32.4 37.2 %copy-start = (f32[512]{0:T(512)S(1)}, f32[512]{0:T(512)}, u32[]{:S(2)}) copy-start(f32[512]{0:T(512)} %param.13) | copy-start | bytes 6148
  94.8 5.3 %collective-permute-start = (bf16[32,512]{1,0:T(8,128)(2,1)}, bf16[32,512]{1,0:T(8,128)(2,1)}, u32[]{:S(2)}, u32[]{:S(2)}) collective-permute-start(bf16[32,512]{1,0:T(8,128)(2,1)} %get-tuple-element.647), channel_id=1, source_target_pairs={{0,16},{1,17},{2,18},{3,19},{4,20},{5,21},{6,22},{7,23},{8,24},{9,... | collective-permute-start | bytes 98312 | tf_op jit(solution)/shard_map/while/body/eval_jaxpr/ppermute | solution.py:13
  126.9 6.0 %collective-permute-start = (bf16[32,512]{1,0:T(8,128)(2,1)}, bf16[32,512]{1,0:T(8,128)(2,1)}, u32[]{:S(2)}, u32[]{:S(2)}) collective-permute-start(bf16[32,512]{1,0:T(8,128)(2,1)} %get-tuple-element.647), channel_id=1, source_target_pairs={{0,16},{1,17},{2,18},{3,19},{4,20},{5,21},{6,22},{7,23},{8,24},{9,... | collective-permute-start | bytes 98312 | tf_op jit(solution)/shard_map/while/body/eval_jaxpr/ppermute | solution.py:13
  158.2 6.1 %collective-permute-start = (bf16[32,512]{1,0:T(8,128)(2,1)}, bf16[32,512]{1,0:T(8,128)(2,1)}, u32[]{:S(2)}, u32[]{:S(2)}) collective-permute-start(bf16[32,512]{1,0:T(8,128)(2,1)} %get-tuple-element.647), channel_id=1, source_target_pairs={{0,16},{1,17},{2,18},{3,19},{4,20},{5,21},{6,22},{7,23},{8,24},{9,... | collective-permute-start | bytes 98312 | tf_op jit(solution)/shard_map/while/body/eval_jaxpr/ppermute | solution.py:13
  191.1 6.0 %collective-permute-start = (bf16[32,512]{1,0:T(8,128)(2,1)}, bf16[32,512]{1,0:T(8,128)(2,1)}, u32[]{:S(2)}, u32[]{:S(2)}) collective-permute-start(bf16[32,512]{1,0:T(8,128)(2,1)} %get-tuple-element.647), channel_id=1, source_target_pairs={{0,16},{1,17},{2,18},{3,19},{4,20},{5,21},{6,22},{7,23},{8,24},{9,... | collective-permute-start | bytes 98312 | tf_op jit(solution)/shard_map/while/body/eval_jaxpr/ppermute | solution.py:13
  222.3 6.1 %collective-permute-start = (bf16[32,512]{1,0:T(8,128)(2,1)}, bf16[32,512]{1,0:T(8,128)(2,1)}, u32[]{:S(2)}, u32[]{:S(2)}) collective-permute-start(bf16[32,512]{1,0:T(8,128)(2,1)} %get-tuple-element.647), channel_id=1, source_target_pairs={{0,16},{1,17},{2,18},{3,19},{4,20},{5,21},{6,22},{7,23},{8,24},{9,... | collective-permute-start | bytes 98312 | tf_op jit(solution)/shard_map/while/body/eval_jaxpr/ppermute | solution.py:13
  266.3 17.8 %all-to-all-start = ((bf16[32,16,512]{2,0,1:T(8,128)(2,1)}), bf16[32,16,512]{2,0,1:T(8,128)(2,1)S(1)}, u32[]{:S(2)}, u32[]{:S(2)}) async-start(bf16[32,16,512]{2,0,1:T(8,128)(2,1)} %bitcast.109), calls=%async_computation | async-start | bytes 1048576 | tf_op jit(solution)/shard_map/while/body/eval_jaxpr/all_to_all | solution.py:101
  284.3 5.8 %collective-permute-start.1 = (bf16[32,512]{1,0:T(8,128)(2,1)S(1)}, bf16[32,512]{1,0:T(8,128)(2,1)S(1)}, u32[]{:S(2)}, u32[]{:S(2)}) collective-permute-start(bf16[32,512]{1,0:T(8,128)(2,1)S(1)} %fusion.38), channel_id=1, source_target_pairs={{16,0},{17,1},{18,2},{19,3},{20,4},{21,5},{22,6},{23,7},{24,8},{25... | collective-permute-start | bytes 98312 | tf_op jit(solution)/shard_map/while/body/eval_jaxpr/ppermute | solution.py:13
  296.9 18.4 %all-to-all-start = ((bf16[32,16,512]{2,0,1:T(8,128)(2,1)}), bf16[32,16,512]{2,0,1:T(8,128)(2,1)S(1)}, u32[]{:S(2)}, u32[]{:S(2)}) async-start(bf16[32,16,512]{2,0,1:T(8,128)(2,1)} %bitcast.109), calls=%async_computation | async-start | bytes 1048576 | tf_op jit(solution)/shard_map/while/body/eval_jaxpr/all_to_all | solution.py:101
  315.5 5.8 %collective-permute-start.1 = (bf16[32,512]{1,0:T(8,128)(2,1)S(1)}, bf16[32,512]{1,0:T(8,128)(2,1)S(1)}, u32[]{:S(2)}, u32[]{:S(2)}) collective-permute-start(bf16[32,512]{1,0:T(8,128)(2,1)S(1)} %fusion.38), channel_id=1, source_target_pairs={{16,0},{17,1},{18,2},{19,3},{20,4},{21,5},{22,6},{23,7},{24,8},{25... | collective-permute-start | bytes 98312 | tf_op jit(solution)/shard_map/while/body/eval_jaxpr/ppermute | solution.py:13
  328.1 18.4 %all-to-all-start = ((bf16[32,16,512]{2,0,1:T(8,128)(2,1)}), bf16[32,16,512]{2,0,1:T(8,128)(2,1)S(1)}, u32[]{:S(2)}, u32[]{:S(2)}) async-start(bf16[32,16,512]{2,0,1:T(8,128)(2,1)} %bitcast.109), calls=%async_computation | async-start | bytes 1048576 | tf_op jit(solution)/shard_map/while/body/eval_jaxpr/all_to_all | solution.py:101
  346.7 5.8 %collective-permute-start.1 = (bf16[32,512]{1,0:T(8,128)(2,1)S(1)}, bf16[32,512]{1,0:T(8,128)(2,1)S(1)}, u32[]{:S(2)}, u32[]{:S(2)}) collective-permute-start(bf16[32,512]{1,0:T(8,128)(2,1)S(1)} %fusion.38), channel_id=1, source_target_pairs={{16,0},{17,1},{18,2},{19,3},{20,4},{21,5},{22,6},{23,7},{24,8},{25... | collective-permute-start | bytes 98312 | tf_op jit(solution)/shard_map/while/body/eval_jaxpr/ppermute | solution.py:13
  359.3 18.4 %all-to-all-start = ((bf16[32,16,512]{2,0,1:T(8,128)(2,1)}), bf16[32,16,512]{2,0,1:T(8,128)(2,1)S(1)}, u32[]{:S(2)}, u32[]{:S(2)}) async-start(bf16[32,16,512]{2,0,1:T(8,128)(2,1)} %bitcast.109), calls=%async_computation | async-start | bytes 1048576 | tf_op jit(solution)/shard_map/while/body/eval_jaxpr/all_to_all | solution.py:101
  377.9 5.8 %collective-permute-start.1 = (bf16[32,512]{1,0:T(8,128)(2,1)S(1)}, bf16[32,512]{1,0:T(8,128)(2,1)S(1)}, u32[]{:S(2)}, u32[]{:S(2)}) collective-permute-start(bf16[32,512]{1,0:T(8,128)(2,1)S(1)} %fusion.38), channel_id=1, source_target_pairs={{16,0},{17,1},{18,2},{19,3},{20,4},{21,5},{22,6},{23,7},{24,8},{25... | collective-permute-start | bytes 98312 | tf_op jit(solution)/shard_map/while/body/eval_jaxpr/ppermute | solution.py:13
  390.5 18.4 %all-to-all-start = ((bf16[32,16,512]{2,0,1:T(8,128)(2,1)}), bf16[32,16,512]{2,0,1:T(8,128)(2,1)S(1)}, u32[]{:S(2)}, u32[]{:S(2)}) async-start(bf16[32,16,512]{2,0,1:T(8,128)(2,1)} %bitcast.109), calls=%async_computation | async-start | bytes 1048576 | tf_op jit(solution)/shard_map/while/body/eval_jaxpr/all_to_all | solution.py:101
  409.1 5.8 %collective-permute-start.1 = (bf16[32,512]{1,0:T(8,128)(2,1)S(1)}, bf16[32,512]{1,0:T(8,128)(2,1)S(1)}, u32[]{:S(2)}, u32[]{:S(2)}) collective-permute-start(bf16[32,512]{1,0:T(8,128)(2,1)S(1)} %fusion.38), channel_id=1, source_target_pairs={{16,0},{17,1},{18,2},{19,3},{20,4},{21,5},{22,6},{23,7},{24,8},{25... | collective-permute-start | bytes 98312 | tf_op jit(solution)/shard_map/while/body/eval_jaxpr/ppermute | solution.py:13
